TPU v7x, 32 devices: a whole 2x2x4 slice. The times are simulated.
32 devices in a mesh: row: 8 (over y, x, core), col: 4 (over z).
Axes of the slice: x: 2, y: 2, z: 4, core: 2. Of those that a mesh axis runs over, the one named last changes fastest.
Arguments:
- density_start: float32 [512, 512], P('row', 'col'), may hold values from -0.5 to 1, as said below
- branches: int32 [6], replicated, may hold values from 0 to 1, as said below
Outputs:
- density: float32 [512, 512], P('row', 'col')
- occupations: float32 [6, 2], replicated
Inputs may be any that keep to these rules, and one draw needn't show every extreme that they name: density_start is symmetric with eigenvalues inside 0 to 1. `branches`: each entry is 0 or 1, and exactly 3 entries are 1.
All inputs are finite; a program needn't handle non-finite values.
Results may differ from a plain program's by a relative error of at most 0.0025.
Values may be sent and summed in bfloat16 or wider, within the bound.
A program may use at most 64 MiB of HBM per device.

v0:
```python
import jax
import jax.numpy as jnp
from jax import lax
from jax.sharding import PartitionSpec as P

ITERS = 6


def taken_in(shard, axis, dim, absorb, state):
    everything = jax.tree.map(lambda a: lax.all_gather(a, axis, axis=dim, tiled=True), shard)
    return absorb(state, everything, jnp.int32(0))


def local_trace(matrix_block, diagonal_mask):
    return jnp.sum(matrix_block * diagonal_mask)


def body(density_start, branches):
    rows_here, cols_here = density_start.shape
    row_first = lax.axis_index("row") * rows_here
    col_first = lax.axis_index("col") * cols_here
    row_ids = row_first + lax.broadcasted_iota(jnp.int32, (rows_here, cols_here), 0)
    col_ids = col_first + lax.broadcasted_iota(jnp.int32, (rows_here, cols_here), 1)
    diagonal_mask = (row_ids == col_ids).astype(jnp.float32)
    size_total = cols_here * lax.axis_size("col")
    density = density_start
    records = []
    for iteration in range(ITERS):
        narrow = density.astype(jnp.bfloat16)
        empty = jnp.zeros((rows_here, cols_here), jnp.float32)
        plain_local = local_trace(density, diagonal_mask)
        row_panel = lax.all_gather(narrow, "col", axis=1, tiled=True)

        def add_rows(accumulated, shard_piece, offset):
            panel_part = lax.dynamic_slice_in_dim(row_panel, offset, shard_piece.shape[0], 1)
            return accumulated + jnp.dot(
                panel_part, shard_piece, preferred_element_type=jnp.float32
            )

        square = taken_in(narrow, "row", 0, add_rows, empty)
        square_local = local_trace(square, diagonal_mask)
        branch_now = branches[iteration]
        records.append(jnp.stack([plain_local, square_local]))
        density = jnp.where(branch_now == 1, 2.0 * density - square, square)
    stacked = jnp.stack(records)
    stacked = lax.psum(stacked, ("row", "col"))
    occupations = stacked / size_total
    return (density, occupations)


def solution(mesh):
    in_specs = (P("row", "col"), P())
    out_specs = (P("row", "col"), P())
    return jax.shard_map(body, mesh=mesh, in_specs=in_specs, out_specs=out_specs, check_vma=False)
```

profile of v0, /device:TPU:0, one launch (start us, length us, event | category | flops | bytes accessed | tf_op | source)
XLA Modules:
  0.0 182.0 jit_solution(16147823306401190443)
XLA Ops:
  0.6 0.0 copy-start
  0.7 1.6 fusion.17
  6.1 0.0 copy-done
  6.1 13.7 %all_gather.36 = bf16[64,512]{1,0:T(8,128)(2,1)S(1)} all-gather(bf16[64,128]{1,0:T(8,128)(2,1)S(1)} %convert_element_type.19), channel_id=1, replica_groups=mesh['row'=8,'col'=4] {'col'}, dimensions={1}, use_global_device_ids=true | all-gather | bytes 81920 | tf_op jit(solution)/shard_map/all_gather | solution.py:32
  19.8 9.2 %all_gather.37 = bf16[512,128]{1,0:T(8,128)(2,1)S(1)} all-gather(bf16[64,128]{1,0:T(8,128)(2,1)S(1)} %convert_element_type.19), channel_id=1, replica_groups=mesh['row'=8,'col'=4] {'row'}, dimensions={0}, use_global_device_ids=true | all-gather | bytes 147456 | tf_op jit(solution)/shard_map/all_gather | solution.py:10
  29.0 0.2 fusion.16
  29.2 12.0 %all_gather.38 = bf16[64,512]{1,0:T(8,128)(2,1)S(1)} all-gather(bf16[64,128]{1,0:T(8,128)(2,1)S(1)} %get-tuple-element.24), channel_id=1, replica_groups=mesh['row'=8,'col'=4] {'col'}, dimensions={1}, use_global_device_ids=true | all-gather | bytes 81920 | tf_op jit(solution)/shard_map/all_gather | solution.py:32
  41.2 9.2 %all_gather.39 = bf16[512,128]{1,0:T(8,128)(2,1)S(1)} all-gather(bf16[64,128]{1,0:T(8,128)(2,1)S(1)} %get-tuple-element.24), channel_id=1, replica_groups=mesh['row'=8,'col'=4] {'row'}, dimensions={0}, use_global_device_ids=true | all-gather | bytes 147456 | tf_op jit(solution)/shard_map/all_gather | solution.py:10
  50.4 0.2 fusion.15
  50.5 12.0 %all_gather.40 = bf16[64,512]{1,0:T(8,128)(2,1)S(1)} all-gather(bf16[64,128]{1,0:T(8,128)(2,1)S(1)} %get-tuple-element.22), channel_id=1, replica_groups=mesh['row'=8,'col'=4] {'col'}, dimensions={1}, use_global_device_ids=true | all-gather | bytes 81920 | tf_op jit(solution)/shard_map/all_gather | solution.py:32
  62.5 8.2 %all_gather.41 = bf16[512,128]{1,0:T(8,128)(2,1)S(1)} all-gather(bf16[64,128]{1,0:T(8,128)(2,1)S(1)} %get-tuple-element.22), channel_id=1, replica_groups=mesh['row'=8,'col'=4] {'row'}, dimensions={0}, use_global_device_ids=true | all-gather | bytes 147456 | tf_op jit(solution)/shard_map/all_gather | solution.py:10
  70.7 0.2 fusion.14
  70.9 12.0 %all_gather.42 = bf16[64,512]{1,0:T(8,128)(2,1)S(1)} all-gather(bf16[64,128]{1,0:T(8,128)(2,1)S(1)} %get-tuple-element.20), channel_id=1, replica_groups=mesh['row'=8,'col'=4] {'col'}, dimensions={1}, use_global_device_ids=true | all-gather | bytes 81920 | tf_op jit(solution)/shard_map/all_gather | solution.py:32
  82.9 9.2 %all_gather.43 = bf16[512,128]{1,0:T(8,128)(2,1)S(1)} all-gather(bf16[64,128]{1,0:T(8,128)(2,1)S(1)} %get-tuple-element.20), channel_id=1, replica_groups=mesh['row'=8,'col'=4] {'row'}, dimensions={0}, use_global_device_ids=true | all-gather | bytes 147456 | tf_op jit(solution)/shard_map/all_gather | solution.py:10
  92.1 0.2 fusion.13
  92.2 12.0 %all_gather.44 = bf16[64,512]{1,0:T(8,128)(2,1)S(1)} all-gather(bf16[64,128]{1,0:T(8,128)(2,1)S(1)} %get-tuple-element.18), channel_id=1, replica_groups=mesh['row'=8,'col'=4] {'col'}, dimensions={1}, use_global_device_ids=true | all-gather | bytes 81920 | tf_op jit(solution)/shard_map/all_gather | solution.py:32
  104.2 8.2 %all_gather.45 = bf16[512,128]{1,0:T(8,128)(2,1)S(1)} all-gather(bf16[64,128]{1,0:T(8,128)(2,1)S(1)} %get-tuple-element.18), channel_id=1, replica_groups=mesh['row'=8,'col'=4] {'row'}, dimensions={0}, use_global_device_ids=true | all-gather | bytes 147456 | tf_op jit(solution)/shard_map/all_gather | solution.py:10
  112.4 0.2 fusion.12
  112.6 12.0 %all_gather.46 = bf16[64,512]{1,0:T(8,128)(2,1)S(1)} all-gather(bf16[64,128]{1,0:T(8,128)(2,1)S(1)} %get-tuple-element.16), channel_id=1, replica_groups=mesh['row'=8,'col'=4] {'col'}, dimensions={1}, use_global_device_ids=true | all-gather | bytes 81920 | tf_op jit(solution)/shard_map/all_gather | solution.py:32
  124.6 9.2 %all_gather.47 = bf16[512,128]{1,0:T(8,128)(2,1)S(1)} all-gather(bf16[64,128]{1,0:T(8,128)(2,1)S(1)} %get-tuple-element.16), channel_id=1, replica_groups=mesh['row'=8,'col'=4] {'row'}, dimensions={0}, use_global_device_ids=true | all-gather | bytes 147456 | tf_op jit(solution)/shard_map/all_gather | solution.py:10
  133.8 1.5 fusion.10
  135.2 1.3 maximum_bitcast_fusion.5
  136.5 0.1 copy.10
  136.6 1.3 maximum_bitcast_fusion.4
  138.0 0.1 copy.9
  138.1 1.3 maximum_bitcast_fusion.3
  139.4 0.1 copy.8
  139.4 1.3 maximum_bitcast_fusion.2
  140.8 0.1 copy.7
  140.9 1.3 maximum_bitcast_fusion.1
  142.2 0.1 copy.6
  142.3 1.3 maximum_bitcast_fusion
  143.6 0.1 copy.5
  143.7 0.1 stack.99
  143.8 37.7 %psum.7 = f32[6,2]{0,1:T(2,128)S(1)} all-reduce(f32[6,2]{0,1:T(2,128)S(1)} %stack.99), channel_id=1, replica_groups=mesh['row'=8,'col'=4] {'row','col'}, use_global_device_ids=true, to_apply=%region_12.13 | all-reduce | flops 12 | bytes 96 | tf_op jit(solution)/shard_map/psum | solution.py:46
  181.5 0.6 broadcast_multiply_fusion
  (3 shorter events, 0.0 us)
Async XLA Ops:
  0.6 5.5 %copy-start = (f32[64,128]{1,0:T(8,128)S(1)}, f32[64,128]{1,0:T(8,128)}, u32[]{:S(2)}) copy-start(f32[64,128]{1,0:T(8,128)} %param.2) | copy-start | bytes 98308
where the time goes:
time: 183 us; the launch traced here: 182 us
  blocking collectives  165 us (90%)
  other arithmetic  8.46 us (5%)
  between operations  4.56 us (2%)
  matrix products  2.26 us (1%)
  local copies, waits for them, and re-layouts  2.23 us (1%)
    all_gather x6, blocking collectives, body(): row_panel = lax.all_gather(narrow, 'col', axis=1, tiled=True)  73.7 us
    all_gather x6, blocking collectives, taken_in(): lax.all_gather(a, axis, axis=dim, tiled=True)  53.2 us
    psum x1, blocking collectives, body(): stacked = lax.psum(stacked, ('row', 'col'))  37.7 us
    another operation x6, other arithmetic, body(): stacked = jnp.stack(records)  7.88 us

commit v1 on v0

--- a/solution.py
+++ b/solution.py
@@ -29,7 +29,9 @@
         narrow = density.astype(jnp.bfloat16)
         empty = jnp.zeros((rows_here, cols_here), jnp.float32)
         plain_local = local_trace(density, diagonal_mask)
-        row_panel = lax.all_gather(narrow, "col", axis=1, tiled=True)
+        row_panel = jnp.concatenate(
+            lax.all_to_all(jnp.stack([narrow] * lax.axis_size("col")), "col", 0, 0), axis=1
+        )
 
         def add_rows(accumulated, shard_piece, offset):
             panel_part = lax.dynamic_slice_in_dim(row_panel, offset, shard_piece.shape[0], 1)

time: 183 us -> 147 us (0.80)
  blocking collectives: 165 us -> 93 us
  starting transfers between devices: 0 us -> 31.9 us
  local copies, waits for them, and re-layouts: 2.23 us -> 5.16 us
    all_gather x6 -> x0, blocking collectives: 73.7 us -> none  [body(): row_panel = lax.all_gather(narrow, 'col', axis=1, tiled=True)]
    all_to_all x0 -> x6, starting transfers between devices: none -> 31.9 us  [body(): lax.all_to_all(jnp.stack([narrow] * lax.axis_size('col')), 'col', 0, 0)]
    another operation x0 -> x6, local copies, waits for them, and re-layouts: none -> 3.8 us  [body(): jnp.stack([narrow] * lax.axis_size('col'))]
    psum x1, blocking collectives: 37.7 us -> 39.8 us  [body(): stacked = lax.psum(stacked, ('row', 'col'))]
  transfers between devices with their start and end apart: 0 -> 6, of which waited for: 0 -> 0; matrix products, arithmetic and copies ran while one was open for 0% -> 0% of each run, Pallas kernels for 0% -> 0%
where the time goes in v1:
time: 147 us; the launch traced here: 146 us
  blocking collectives  93 us (63%)
  starting transfers between devices  31.9 us (22%)
  other arithmetic  9.29 us (6%)
  local copies, waits for them, and re-layouts  5.16 us (4%)
  between operations  4.46 us (3%)
  matrix products  2.27 us (2%)
    all_gather x6, blocking collectives, taken_in(): lax.all_gather(a, axis, axis=dim, tiled=True)  53.2 us
    psum x1, blocking collectives, body(): stacked = lax.psum(stacked, ('row', 'col'))  39.8 us
    all_to_all x6, starting transfers between devices, body(): lax.all_to_all(jnp.stack([narrow] * lax.axis_size('col')), 'col', 0, 0)  31.9 us
    another operation x6, other arithmetic, body(): stacked = jnp.stack(records)  7.96 us
    another operation x6, local copies, waits for them, and re-layouts, body(): jnp.stack([narrow] * lax.axis_size('col'))  3.8 us
  transfers between devices with their start and end apart: 6, of which 0 were waited for; matrix products, arithmetic and copies ran while one was open for 0% of the time, Pallas kernels for 0%

profile of v1, /device:TPU:0, one launch (start us, length us, event | category | flops | bytes accessed | tf_op | source)
XLA Modules:
  0.0 146.1 jit_solution(2799619118825802830)
XLA Ops:
  0.6 0.8 convert_element_type.19
  1.4 0.6 stack.117
  2.0 0.0 copy-start.1
  2.0 6.5 %all-to-all-start = ((bf16[4,64,128]{2,1,0:T(8,128)(2,1)}), bf16[4,64,128]{2,1,0:T(8,128)(2,1)S(1)}, u32[]{:S(2)}, u32[]{:S(2)}) async-start(bf16[4,64,128]{2,1,0:T(8,128)(2,1)} %stack.117), calls=%async_computation | async-start | bytes 131072 | tf_op jit(solution)/shard_map/all_to_all | solution.py:33
  8.5 0.0 copy-done.1
  8.5 0.7 fusion.35
  9.9 0.0 copy-start
  9.9 9.2 %all_gather.18 = bf16[512,128]{1,0:T(8,128)(2,1)S(1)} all-gather(bf16[64,128]{1,0:T(8,128)(2,1)S(1)} %convert_element_type.19), channel_id=1, replica_groups=mesh['row'=8,'col'=4] {'row'}, dimensions={0}, use_global_device_ids=true | all-gather | bytes 147456 | tf_op jit(solution)/shard_map/all_gather | solution.py:10
  19.1 0.0 all-to-all-done
  19.1 0.0 copy-done
  19.1 0.2 fusion.34
  19.3 0.6 stack.118
  19.9 5.1 %all-to-all-start.1 = ((bf16[4,64,128]{2,1,0:T(8,128)(2,1)}), bf16[4,64,128]{2,1,0:T(8,128)(2,1)S(1)}, u32[]{:S(2)}, u32[]{:S(2)}) async-start(bf16[4,64,128]{2,1,0:T(8,128)(2,1)} %stack.118), calls=%async_computation.1 | async-start | bytes 131072 | tf_op jit(solution)/shard_map/all_to_all | solution.py:33
  25.6 9.2 %all_gather.19 = bf16[512,128]{1,0:T(8,128)(2,1)S(1)} all-gather(bf16[64,128]{1,0:T(8,128)(2,1)S(1)} %get-tuple-element.26), channel_id=1, replica_groups=mesh['row'=8,'col'=4] {'row'}, dimensions={0}, use_global_device_ids=true | all-gather | bytes 147456 | tf_op jit(solution)/shard_map/all_gather | solution.py:10
  34.8 0.0 all-to-all-done.1
  34.8 0.2 fusion.33
  34.9 0.6 stack.119
  35.6 5.1 %all-to-all-start.2 = ((bf16[4,64,128]{2,1,0:T(8,128)(2,1)}), bf16[4,64,128]{2,1,0:T(8,128)(2,1)S(1)}, u32[]{:S(2)}, u32[]{:S(2)}) async-start(bf16[4,64,128]{2,1,0:T(8,128)(2,1)} %stack.119), calls=%async_computation.2 | async-start | bytes 131072 | tf_op jit(solution)/shard_map/all_to_all | solution.py:33
  41.3 8.2 %all_gather.20 = bf16[512,128]{1,0:T(8,128)(2,1)S(1)} all-gather(bf16[64,128]{1,0:T(8,128)(2,1)S(1)} %get-tuple-element.24), channel_id=1, replica_groups=mesh['row'=8,'col'=4] {'row'}, dimensions={0}, use_global_device_ids=true | all-gather | bytes 147456 | tf_op jit(solution)/shard_map/all_gather | solution.py:10
  49.5 0.0 all-to-all-done.2
  49.5 0.2 fusion.32
  49.7 0.6 stack.120
  50.3 5.1 %all-to-all-start.3 = ((bf16[4,64,128]{2,1,0:T(8,128)(2,1)}), bf16[4,64,128]{2,1,0:T(8,128)(2,1)S(1)}, u32[]{:S(2)}, u32[]{:S(2)}) async-start(bf16[4,64,128]{2,1,0:T(8,128)(2,1)} %stack.120), calls=%async_computation.3 | async-start | bytes 131072 | tf_op jit(solution)/shard_map/all_to_all | solution.py:33
  57.3 9.2 %all_gather.21 = bf16[512,128]{1,0:T(8,128)(2,1)S(1)} all-gather(bf16[64,128]{1,0:T(8,128)(2,1)S(1)} %get-tuple-element.22), channel_id=1, replica_groups=mesh['row'=8,'col'=4] {'row'}, dimensions={0}, use_global_device_ids=true | all-gather | bytes 147456 | tf_op jit(solution)/shard_map/all_gather | solution.py:10
  66.5 0.0 all-to-all-done.3
  66.5 0.2 fusion.31
  66.7 0.6 stack.121
  67.3 5.1 %all-to-all-start.4 = ((bf16[4,64,128]{2,1,0:T(8,128)(2,1)}), bf16[4,64,128]{2,1,0:T(8,128)(2,1)S(1)}, u32[]{:S(2)}, u32[]{:S(2)}) async-start(bf16[4,64,128]{2,1,0:T(8,128)(2,1)} %stack.121), calls=%async_computation.4 | async-start | bytes 131072 | tf_op jit(solution)/shard_map/all_to_all | solution.py:33
  72.4 8.2 %all_gather.22 = bf16[512,128]{1,0:T(8,128)(2,1)S(1)} all-gather(bf16[64,128]{1,0:T(8,128)(2,1)S(1)} %get-tuple-element.20), channel_id=1, replica_groups=mesh['row'=8,'col'=4] {'row'}, dimensions={0}, use_global_device_ids=true | all-gather | bytes 147456 | tf_op jit(solution)/shard_map/all_gather | solution.py:10
  80.6 0.0 all-to-all-done.4
  80.6 0.2 fusion.30
  80.8 0.6 stack.122
  81.4 5.1 %all-to-all-start.5 = ((bf16[4,64,128]{2,1,0:T(8,128)(2,1)}), bf16[4,64,128]{2,1,0:T(8,128)(2,1)S(1)}, u32[]{:S(2)}, u32[]{:S(2)}) async-start(bf16[4,64,128]{2,1,0:T(8,128)(2,1)} %stack.122), calls=%async_computation.5 | async-start | bytes 131072 | tf_op jit(solution)/shard_map/all_to_all | solution.py:33
  86.5 9.2 %all_gather.23 = bf16[512,128]{1,0:T(8,128)(2,1)S(1)} all-gather(bf16[64,128]{1,0:T(8,128)(2,1)S(1)} %get-tuple-element.18), channel_id=1, replica_groups=mesh['row'=8,'col'=4] {'row'}, dimensions={0}, use_global_device_ids=true | all-gather | bytes 147456 | tf_op jit(solution)/shard_map/all_gather | solution.py:10
  95.7 0.0 all-to-all-done.5
  95.7 1.5 %fusion.28 = (f32[]{:T(128)}, f32[]{:T(128)}, f32[]{:T(128)}, f32[]{:T(128)}, f32[]{:T(128)}, /*index=5*/f32[]{:T(128)}, f32[]{:T(128)}, f32[]{:T(128)}, f32[]{:...) fusion(f32[64,128]{1,0:T(8,128)S(1)} %get-tuple-element.19, s32[128]{0:T(128)S(1)} %iota_add_fusion, ...), kind=kOutput, calls=%fused_computation.46 | convolution fusion | flops 8617972 | bytes 590641 | tf_op jit(solution)/shard_map/dot_general | solution.py:38
  97.2 1.4 maximum_bitcast_fusion.5
  98.6 0.1 copy.17
  98.7 1.3 maximum_bitcast_fusion.4
  99.9 0.1 copy.16
  100.0 1.3 maximum_bitcast_fusion.3
  101.4 0.1 copy.15
  101.5 1.3 maximum_bitcast_fusion.2
  102.8 0.1 copy.14
  102.9 1.3 maximum_bitcast_fusion.1
  104.2 0.1 copy.13
  104.3 1.3 maximum_bitcast_fusion
  105.6 0.1 copy.12
  105.7 0.1 stack.147
  105.8 39.8 %psum.7 = f32[6,2]{0,1:T(2,128)S(1)} all-reduce(f32[6,2]{0,1:T(2,128)S(1)} %stack.147), channel_id=1, replica_groups=mesh['row'=8,'col'=4] {'row','col'}, use_global_device_ids=true, to_apply=%region_12.13 | all-reduce | flops 12 | bytes 96 | tf_op jit(solution)/shard_map/psum | solution.py:48
  145.6 0.6 broadcast_multiply_fusion
  (2 shorter events, 0.0 us)
Async XLA Ops:
  2.0 6.5 %copy-start.1 = (s32[6]{0:T(128)S(1)}, s32[6]{0:T(128)}, u32[]{:S(2)}) copy-start(s32[6]{0:T(128)} %param.3) | copy-start | bytes 76
  2.0 17.1 %all-to-all-start = ((bf16[4,64,128]{2,1,0:T(8,128)(2,1)}), bf16[4,64,128]{2,1,0:T(8,128)(2,1)S(1)}, u32[]{:S(2)}, u32[]{:S(2)}) async-start(bf16[4,64,128]{2,1,0:T(8,128)(2,1)} %stack.117), calls=%async_computation | async-start | bytes 131072 | tf_op jit(solution)/shard_map/all_to_all | solution.py:33
  9.9 9.2 %copy-start = (f32[64,128]{1,0:T(8,128)S(1)}, f32[64,128]{1,0:T(8,128)}, u32[]{:S(2)}) copy-start(f32[64,128]{1,0:T(8,128)} %param.2) | copy-start | bytes 98308
  19.9 14.8 %all-to-all-start.1 = ((bf16[4,64,128]{2,1,0:T(8,128)(2,1)}), bf16[4,64,128]{2,1,0:T(8,128)(2,1)S(1)}, u32[]{:S(2)}, u32[]{:S(2)}) async-start(bf16[4,64,128]{2,1,0:T(8,128)(2,1)} %stack.118), calls=%async_computation.1 | async-start | bytes 131072 | tf_op jit(solution)/shard_map/all_to_all | solution.py:33
  35.6 14.0 %all-to-all-start.2 = ((bf16[4,64,128]{2,1,0:T(8,128)(2,1)}), bf16[4,64,128]{2,1,0:T(8,128)(2,1)S(1)}, u32[]{:S(2)}, u32[]{:S(2)}) async-start(bf16[4,64,128]{2,1,0:T(8,128)(2,1)} %stack.119), calls=%async_computation.2 | async-start | bytes 131072 | tf_op jit(solution)/shard_map/all_to_all | solution.py:33
  50.3 16.2 %all-to-all-start.3 = ((bf16[4,64,128]{2,1,0:T(8,128)(2,1)}), bf16[4,64,128]{2,1,0:T(8,128)(2,1)S(1)}, u32[]{:S(2)}, u32[]{:S(2)}) async-start(bf16[4,64,128]{2,1,0:T(8,128)(2,1)} %stack.120), calls=%async_computation.3 | async-start | bytes 131072 | tf_op jit(solution)/shard_map/all_to_all | solution.py:33
  67.3 13.3 %all-to-all-start.4 = ((bf16[4,64,128]{2,1,0:T(8,128)(2,1)}), bf16[4,64,128]{2,1,0:T(8,128)(2,1)S(1)}, u32[]{:S(2)}, u32[]{:S(2)}) async-start(bf16[4,64,128]{2,1,0:T(8,128)(2,1)} %stack.121), calls=%async_computation.4 | async-start | bytes 131072 | tf_op jit(solution)/shard_map/all_to_all | solution.py:33
  81.4 14.3 %all-to-all-start.5 = ((bf16[4,64,128]{2,1,0:T(8,128)(2,1)}), bf16[4,64,128]{2,1,0:T(8,128)(2,1)S(1)}, u32[]{:S(2)}, u32[]{:S(2)}) async-start(bf16[4,64,128]{2,1,0:T(8,128)(2,1)} %stack.122), calls=%async_computation.5 | async-start | bytes 131072 | tf_op jit(solution)/shard_map/all_to_all | solution.py:33
